TPU v7x, 32 devices: a whole 2x2x4 slice. The times are simulated.
32 devices in a mesh: clip: 2 (over core), ha: 4 (over y, x), wa: 4 (over z).
Axes of the slice: x: 2, y: 2, z: 4, core: 2. Of those that a mesh axis runs over, the one named last changes fastest.
Arguments:
- frames: bfloat16 [8, 96, 128, 128], P('clip', 'ha', 'wa'), parts along dimension 0, may hold values from -60 to 60, as said below
- caches: bfloat16 [4, 4, 96, 128, 128], P('clip', None, 'ha', 'wa'), parts along dimension 0, may hold values from -4 to 4
- conv_weights: bfloat16 [4, 3, 3, 3, 128, 128], replicated, may hold values from -0.109375 to 0.109375
- conv_bias: float32 [4, 128], replicated, may hold values from -3 to 3
- norm_gain: float32 [4, 128], replicated, may hold values from 0.25 to 1.75
- norm_shift: float32 [4, 128], replicated, may hold values from -3 to 3
Outputs:
- encoded: bfloat16 [8, 96, 128, 128], P('clip', 'ha', 'wa'), parts along dimension 0
- new_caches: bfloat16 [4, 4, 96, 128, 128], P('clip', None, 'ha', 'wa'), parts along dimension 0
There are 2 independent parts, one for each index of `clip`. A program takes and returns all parts, laid end to end along the dimension named above; an argument that names none is the same for every part. Nothing has to cross between parts.
Inputs may be any that keep to these rules, and one draw needn't show every extreme that they name: `frames`: real-valued features.
All inputs are finite; a program needn't handle non-finite values.
Results may differ from a plain program's by a relative error of at most 0.005.
Values may be sent and summed in bfloat16 or wider, within the bound.
A program may use at most 64 MiB of HBM per device.

v0:
```python
import functools

import jax
import jax.numpy as jnp
from jax import lax
from jax.experimental import pallas as pl
from jax.experimental.pallas import tpu as pltpu
from jax.sharding import PartitionSpec as P

GROUPS = 32
EPSILON = 1e-06
MESH = pl.DeviceIdType.MESH
F32 = jnp.float32
BF16 = jnp.bfloat16
ROW_BLOCK = 12
DIRECTIONS = [(dy, dx) for dy in (-1, 0, 1) for dx in (-1, 0, 1) if (dy, dx) != (0, 0)]


def kernel(dims, *refs):
    (frames, caches, weights, bias, gain, shift, encoded, kept,
     x, cb, v, vc, a, t, acc, y,
     s_out, s_in,
     lr_out, lc_out, lk_out, lr_in, lc_in, lk_in,
     cr_out, cc_out, ck_out, cr_in, cc_in, ck_in,
     load_sem, weight_sem, kept_sem, out_sem,
     stat_send, stat_recv, halo_send, halo_recv) = refs
    nh, nw, fr, cf, convs, h, w, c = dims
    pitch = w + 8
    peers = nh * nw
    cell_count = fr * h * w * peers * (c // GROUPS)
    clip, ha, wa = lax.axis_index("clip"), lax.axis_index("ha"), lax.axis_index("wa")
    me = ha * nw + wa
    others = [
        (lax.rem(ha + i, nh), lax.rem(wa + j, nw))
        for i in range(nh)
        for j in range(nw)
        if (i, j) != (0, 0)
    ]
    barrier = pltpu.get_barrier_semaphore()
    for ph, pw in others:
        pl.semaphore_signal(barrier, inc=1, device_id=(clip, ph, pw), device_id_type=MESH)

    load_x = pltpu.make_async_copy(frames, x, load_sem.at[0])
    load_x.start()
    load_c = pltpu.make_async_copy(caches, cb, load_sem.at[1])
    load_c.start()

    def weight_copies(k):
        copies = []
        for dt in range(3):
            for half in range(2):
                copies.append(
                    pltpu.make_async_copy(
                        weights.at[k, dt],
                        t.at[k, dt + half, :, :, pl.ds(half * c, c)],
                        weight_sem.at[k, dt * 2 + half],
                    )
                )
        return copies

    for copy in weight_copies(0):
        copy.start()

    def zero_weights(k, carry):
        t[k, 3, :, :, 0:c] = jnp.zeros((3, 3 * c, c), BF16)
        t[k, 0, :, :, c : 2 * c] = jnp.zeros((3, 3 * c, c), BF16)
        return carry

    lax.fori_loop(0, convs, zero_weights, 0)

    def exists(dy, dx):
        conds = []
        if dy:
            conds.append(ha > 0 if dy < 0 else ha < nh - 1)
        if dx:
            conds.append(wa > 0 if dx < 0 else wa < nw - 1)
        return conds[0] if len(conds) == 1 else jnp.logical_and(*conds)

    parts = fr // 2

    def halo_copy(live, k, part, dy, dx, towards):
        e = k * parts + part if live else convs * parts + k
        span = pl.ds(2 * part, 2) if live else pl.ds(0, cf)
        rows_out, rows_in = (lr_out, lr_in) if live else (cr_out, cr_in)
        cols_out, cols_in = (lc_out, lc_in) if live else (cc_out, cc_in)
        ends_out, ends_in = (lk_out, lk_in) if live else (ck_out, ck_in)
        if dx == 0:
            src = rows_out.at[k, int(dy > 0), span]
            dst = rows_in.at[k, int(dy < 0), span]
        elif dy == 0:
            src = cols_out.at[k, int(dx > 0), span]
            dst = cols_in.at[k, int(dx < 0), span]
        else:
            index = int(dy > 0) * 2 + int(dx > 0)
            src = ends_out.at[k, index, span]
            dst = ends_in.at[k, 3 - index, span]
        d = DIRECTIONS.index((dy, dx))
        back = DIRECTIONS.index((-dy, -dx))
        return pltpu.make_async_remote_copy(
            src_ref=src,
            dst_ref=dst,
            send_sem=halo_send.at[e, d],
            recv_sem=halo_recv.at[e, back],
            device_id=(clip, ha + dy * towards, wa + dx * towards),
            device_id_type=MESH,
        )

    def pack_edges(live, k, part):
        field = v if live else vc.at[k]
        rows_out = lr_out if live else cr_out
        cols_out = lc_out if live else cc_out
        ends_out = lk_out if live else ck_out
        for f in range(2 * part, 2 * part + 2) if live else range(cf):
            for side in range(2):
                first = side * (w - 1)
                top = side * (h - 1) * w
                rows_out[k, side, f] = field[f, top : top + w, :].astype(BF16)
                cols_out[k, side, f] = field[f, pl.ds(first, h, stride=w), :].astype(BF16)
                for low in range(2):
                    row = low * (h - 1) * w + first
                    ends_out[k, low * 2 + side, f] = field[f, row : row + 1, :]

    def send_halo(live, k, part):
        pack_edges(live, k, part)
        for dy, dx in DIRECTIONS:

            @pl.when(exists(dy, dx))
            def _():
                halo_copy(live, k, part, dy, dx, 1).start()

    def wait_halo(live, k):
        for dy, dx in DIRECTIONS:

            @pl.when(exists(dy, dx))
            def _():
                for part in range(parts if live else 1):
                    halo_copy(live, k, part, -dy, -dx, -1).wait_recv()

    def wait_sent(live, k):
        for dy, dx in DIRECTIONS:

            @pl.when(exists(dy, dx))
            def _():
                for part in range(parts if live else 1):
                    halo_copy(live, k, part, dy, dx, 1).wait_send()

    def stat_copy(k, number, sender):
        ph, pw = others[number]
        return pltpu.make_async_remote_copy(
            src_ref=s_out.at[k],
            dst_ref=s_in.at[k, sender],
            send_sem=stat_send.at[k, number],
            recv_sem=stat_recv.at[k, sender],
            device_id=(clip, ph, pw),
            device_id_type=MESH,
        )

    def send_stats(k, sums, squares):
        both = jnp.concatenate(
            [jnp.sum(sums, axis=0, keepdims=True), jnp.sum(squares, axis=0, keepdims=True)], axis=0
        )
        s_out[k] = both
        s_in[k, me] = both
        for number in range(peers - 1):
            stat_copy(k, number, me).start()

    def wait_stats(k):
        for number, (ph, pw) in enumerate(others):
            stat_copy(k, number, ph * nw + pw).wait_recv()
        total = s_in[k, 0]
        for i in range(1, peers):
            total = total + s_in[k, i]
        total = jnp.concatenate([total, jnp.zeros((6, c), F32)], axis=0)
        lane = lax.broadcasted_iota(jnp.int32, (8, c), 1)
        step = 1
        while step < c // GROUPS:
            total = total + jnp.where(
                lax.rem(lane, 2 * step) < step,
                pltpu.roll(total, c - step, 1),
                pltpu.roll(total, step, 1),
            )
            step *= 2
        mean = total[0:1] / cell_count
        variance = total[1:2] / cell_count - mean * mean
        multiplier = lax.rsqrt(variance + EPSILON) * gain[k : k + 1, :]
        offset = shift[k : k + 1, :] - mean * multiplier
        return multiplier, offset

    def silu(values):
        half = 0.5 * values
        return half + half * jnp.tanh(half)

    def build(par, f, row_of, rows, cols, ends):
        for r in range(h + 2):
            cells = rows[0]() if r == 0 else rows[1]() if r == h + 1 else row_of(r - 1)
            a[par, f, r, :, c : 2 * c] = cells.astype(BF16)
            y[r * pitch + 1 : r * pitch + 1 + w, :] = cells
        for side in range(2):
            edge = side * (w + 1)
            y[pl.ds(pitch + edge, h, stride=pitch), :] = cols[side]()
            for low in range(2):
                at = low * (h + 1) * pitch + edge
                y[at : at + 1, :] = ends[low * 2 + side]()
        for r in range(h + 2):
            for dw in (0, 2):
                at = r * pitch + dw
                a[par, f, r, :, dw * c : (dw + 1) * c] = y[at : at + w, :].astype(BF16)

    def masked(dy, dx, values):
        return jnp.where(exists(dy, dx), values, 0.0)

    SIDE = (-1, 1)

    def build_cached(k):
        par = k % 2

        def body(f, carry):
            build(
                par,
                f,
                lambda r: vc[k, f, r * w : (r + 1) * w, :],
                [lambda i=i: masked(SIDE[i], 0, cr_in[k, i, f].astype(F32)) for i in range(2)],
                [lambda i=i: masked(0, SIDE[i], cc_in[k, i, f].astype(F32)) for i in range(2)],
                [lambda i=i: masked(SIDE[i // 2], SIDE[i % 2], ck_in[k, i, f]) for i in range(4)],
            )
            return carry

        lax.fori_loop(0, cf, body, 0)

    def build_live(k, multiplier, offset):
        par = k % 2

        def act(values):
            return silu(values * multiplier + offset)

        def body(f, carry):
            build(
                par,
                cf + f,
                lambda r: act(v[f, r * w : (r + 1) * w, :]),
                [lambda i=i: masked(SIDE[i], 0, act(lr_in[k, i, f].astype(F32))) for i in range(2)],
                [lambda i=i: masked(0, SIDE[i], act(lc_in[k, i, f].astype(F32))) for i in range(2)],
                [
                    lambda i=i: masked(SIDE[i // 2], SIDE[i % 2], act(lk_in[k, i, f]))
                    for i in range(4)
                ],
            )
            return carry

        lax.fori_loop(0, fr, body, 0)

    def product(k, first, low, high, block):
        par = k % 2
        pieces = []
        for f in range(low, high):
            for dh in range(3):
                piece = a[par, first + f, pl.ds(block * ROW_BLOCK + dh, ROW_BLOCK)]
                pieces.append(piece.reshape(ROW_BLOCK * w, 3 * c))
        left = jnp.concatenate(pieces, axis=1)
        right = t[k, low:high].reshape((high - low) * 9 * c, 2 * c)
        return jnp.dot(left, right, preferred_element_type=F32)

    blocks = h // ROW_BLOCK
    cells = ROW_BLOCK * w

    def conv_cached(k):
        def body(block, carry):
            acc[pl.ds(pl.multiple_of(block * cells, cells), cells), :] = product(k, 0, 0, cf, block)
            return carry

        lax.fori_loop(0, blocks, body, 0)

    def conv_live(k):
        bias_row = bias[k : k + 1, :]
        zero = jnp.zeros((8, c), F32)
        carry = (zero, zero)
        for pair in range(fr // 2):

            def body(block, carry, pair=pair):
                sums, squares = carry
                span = pl.ds(pl.multiple_of(block * cells, cells), cells)
                if pair == 0:
                    both = product(k, 0, cf, cf + 2, block) + acc[span, :]
                else:
                    both = product(k, 2 * pair, 0, 4, block)
                for half in range(2):
                    f = 2 * pair + half
                    result = both[:, half * c : (half + 1) * c] + bias_row
                    if k % 2:
                        rounded = (x[f, span, :].astype(F32) + result).astype(BF16)
                        x[f, span, :] = rounded
                        result = rounded.astype(F32)
                    if k < convs - 1:
                        v[f, span, :] = result
                        slabs = result.reshape(cells // 8, 8, c)
                        sums = sums + jnp.sum(slabs, axis=0)
                        squares = squares + jnp.sum(slabs * slabs, axis=0)
                return sums, squares

            carry = lax.fori_loop(0, blocks, body, carry)
            if k == convs - 1:
                out_copy(pair).start()
            elif pair < parts - 1:
                send_halo(True, k + 1, pair)
        return carry

    def out_copy(pair):
        span = pl.ds(2 * pair, 2)
        return pltpu.make_async_copy(x.at[span], encoded.at[span], out_sem.at[pair])

    def kept_copy(k):
        return pltpu.make_async_copy(
            a.at[k % 2, pl.ds(fr, cf), pl.ds(1, h), :, pl.ds(c, c)], kept.at[:, k], kept_sem.at[k]
        )

    def settle(k):
        wait_sent(True, k)
        wait_sent(False, k)
        for number in range(peers - 1):
            stat_copy(k, number, me).wait_send()

    load_x.wait()

    def widen(f, carry):
        sums, squares = carry
        values = x[f].astype(F32)
        v[f] = values
        slabs = values.reshape(h * w // 8, 8, c)
        return sums + jnp.sum(slabs, axis=0), squares + jnp.sum(slabs * slabs, axis=0)

    zero = jnp.zeros((8, c), F32)
    carry = lax.fori_loop(0, fr, widen, (zero, zero))
    pl.semaphore_wait(barrier, peers - 1)
    send_stats(0, *carry)
    for part in range(parts):
        send_halo(True, 0, part)

    def send_cached(k):
        def widen_cache(f, carry):
            vc[k, f] = cb[f, k].astype(F32)
            return carry

        lax.fori_loop(0, cf, widen_cache, 0)
        send_halo(False, k, 0)

    load_c.wait()
    send_cached(0)
    for k in range(convs):
        if k >= 2:
            kept_copy(k - 2).wait()
        wait_halo(False, k)
        build_cached(k)
        for copy in weight_copies(k):
            copy.wait()
        conv_cached(k)
        if k < convs - 1:
            for copy in weight_copies(k + 1):
                copy.start()
            send_cached(k + 1)
        if k:
            settle(k - 1)
        multiplier, offset = wait_stats(k)
        wait_halo(True, k)
        build_live(k, multiplier, offset)
        kept_copy(k).start()
        carry = conv_live(k)
        if k < convs - 1:
            send_stats(k + 1, *carry)
            send_halo(True, k + 1, parts - 1)

    settle(convs - 1)
    for k in range(max(convs - 2, 0), convs):
        kept_copy(k).wait()
    for pair in range(parts):
        out_copy(pair).wait()


def local(nh, nw, frames, caches, conv_weights, conv_bias, norm_gain, norm_shift):
    fr, h, w, c = frames.shape
    cf, convs = caches.shape[:2]
    dims = (nh, nw, fr, cf, convs, h, w, c)
    peers = nh * nw
    vmem = pltpu.VMEM
    dma = pltpu.SemaphoreType.DMA
    scratch = [
        vmem((fr, h * w, c), BF16),
        vmem((cf, convs, h * w, c), BF16),
        vmem((fr, h * w, c), F32),
        vmem((convs, cf, h * w, c), F32),
        vmem((2, fr + cf, h + 2, w, 3 * c), BF16),
        vmem((convs, 4, 3, 3 * c, 2 * c), BF16),
        vmem((h * w, 2 * c), F32),
        vmem(((h + 2) * (w + 8), c), F32),
        vmem((convs, 2, c), F32),
        vmem((convs, peers, 2, c), F32),
    ]
    for nf in (fr, cf):
        scratch += [
            vmem((convs, 2, nf, w, c), BF16),
            vmem((convs, 2, nf, h, c), BF16),
            vmem((convs, 4, nf, 1, c), F32),
            vmem((convs, 2, nf, w, c), BF16),
            vmem((convs, 2, nf, h, c), BF16),
            vmem((convs, 4, nf, 1, c), F32),
        ]
    scratch += [
        dma((2,)),
        dma((convs, 6)),
        dma((convs,)),
        dma((fr // 2,)),
        dma((convs, peers - 1)),
        dma((convs, peers)),
        dma((convs * (fr // 2 + 1), 8)),
        dma((convs * (fr // 2 + 1), 8)),
    ]
    anywhere = pl.BlockSpec(memory_space=pl.ANY)
    inside = pl.BlockSpec(memory_space=pltpu.VMEM)
    encoded, kept = pl.pallas_call(
        functools.partial(kernel, dims),
        out_shape=(
            jax.ShapeDtypeStruct((fr, h * w, c), BF16),
            jax.ShapeDtypeStruct(caches.shape, BF16),
        ),
        in_specs=[anywhere] * 3 + [inside] * 3,
        out_specs=(anywhere, anywhere),
        scratch_shapes=scratch,
        compiler_params=pltpu.CompilerParams(
            collective_id=0, has_side_effects=True, vmem_limit_bytes=56 * 1024 * 1024
        ),
    )(
        frames.reshape(fr, h * w, c),
        caches.reshape(cf, convs, h * w, c),
        conv_weights.reshape(convs, 3, 3, 3 * c, c),
        conv_bias,
        norm_gain,
        norm_shift,
    )
    return encoded.reshape(frames.shape), kept


def solution(mesh):
    return jax.shard_map(
        functools.partial(local, mesh.shape["ha"], mesh.shape["wa"]),
        mesh=mesh,
        in_specs=(
            P("clip", "ha", "wa", None),
            P("clip", None, "ha", "wa", None),
            P(),
            P(),
            P(),
            P(),
        ),
        out_specs=(P("clip", "ha", "wa", None), P("clip", None, "ha", "wa", None)),
        check_vma=False,
    )
```

profile of v0, /device:TPU:0, one launch (start us, length us, event | category | flops | bytes accessed | tf_op | source)
XLA Modules:
  0.0 50.9 jit_solution(17239416024005400564)
XLA Ops:
  0.6 47.0 %shard_map.77 = (bf16[4,768,128]{2,1,0:T(8,128)(2,1)}, bf16[2,4,24,32,128]{4,3,2,1,0:T(8,128)(2,1)}) custom-call(bf16[4,768,128]{2,1,0:T(8,128)(2,1)} %bitcast.6, bf16[2,4,768,128]{3,2,1,0:T(8,128)(2,1)} %bitcast.5, bf16[4,3,3,384,128]{4,3,2,1,0:T(8,128)(2,1)} %bitcast.4, f32[4,128]{1,0:T(4,128)} %refs_3_.1, f32[4,128]{1,0:T(4,128)} %refs_4_.1, f32[4,128]{1,0:T(4,128)} %refs_5_.1), custom_call_target="tpu_custom_call" | custom-call | tf_op jit(solution)/shard_map/pallas_call | solution.py:418
  47.6 0.0 copy-start
  47.6 2.2 %copy.10 = bf16[4,24,32,128]{3,2,1,0:T(8,128)(2,1)} copy(bf16[4,24,32,128]{3,2,1,0:T(8,128)(2,1)} %bitcast.7) | data formatting | bytes 1572864
  49.8 0.0 copy-done
  49.8 1.1 %copy.11 = bf16[2,4,24,32,128]{4,3,2,1,0:T(8,128)(2,1)} copy(bf16[2,4,24,32,128]{4,3,2,1,0:T(8,128)(2,1)S(1)} %copy-done) | data formatting | bytes 3145728
Async XLA Ops:
  47.6 2.2 %copy-start = (bf16[2,4,24,32,128]{4,3,2,1,0:T(8,128)(2,1)S(1)}, bf16[2,4,24,32,128]{4,3,2,1,0:T(8,128)(2,1)}, u32[]{:S(2)}) copy-start(bf16[2,4,24,32,128]{4,3,2,1,0:T(8,128)(2,1)} %get-tuple-element.9) | copy-start | bytes 4718596
where the time goes:
time: 51.1 us; the launch traced here: 50.9 us
  Pallas kernels  47 us (92%)
  local copies, waits for them, and re-layouts  3.33 us (7%)
  between operations  0.65 us (1%)
    pallas_call x1, Pallas kernels, local(): pl.pallas_call(functools.partial(kernel, dims), out_shape=(jax.ShapeDtype...  47 us
    unnamed x4, local copies, waits for them, and re-layouts  3.33 us

commit v1 on v0

v1 whole, which is shorter than its diff:
```python
import functools

import jax
import jax.numpy as jnp
from jax import lax
from jax.experimental import pallas as pl
from jax.experimental.pallas import tpu as pltpu
from jax.sharding import PartitionSpec as P

GROUPS = 32
EPSILON = 1e-06
MESH = pl.DeviceIdType.MESH
F32 = jnp.float32
BF16 = jnp.bfloat16
DIRECTIONS = [(dy, dx) for dy in (-1, 0, 1) for dx in (-1, 0, 1) if (dy, dx) != (0, 0)]
SIDE = (-1, 1)
LEAD = 8
POINTS = 4
PLANES = 4


def silu_of_half(half):
    return half + half * jnp.tanh(half)


def exists_at(nh, nw):
    ha, wa = lax.axis_index("ha"), lax.axis_index("wa")

    def exists(dy, dx):
        conds = []
        if dy:
            conds.append(ha > 0 if dy < 0 else ha < nh - 1)
        if dx:
            conds.append(wa > 0 if dx < 0 else wa < nw - 1)
        return conds[0] if len(conds) == 1 else jnp.logical_and(*conds)

    return exists


def build(s, d, h, w, c, row_of, rows, cols, ends):
    pitch = w + 2 * LEAD
    half = w // 2
    for r in range(h + 2):
        cells = rows[0]() if r == 0 else rows[1]() if r == h + 1 else row_of(r - 1)
        at = r * pitch + LEAD
        s[at : at + w, :] = cells
    for side in range(2):
        edge = LEAD - 1 + side * (w + 1)
        s[pl.ds(pitch + edge, h, stride=pitch), :] = cols[side]()
        for low in range(2):
            at = low * (h + 1) * pitch + edge
            s[at : at + 1, :] = ends[low * 2 + side]()

    def planes(r):
        return [
            s[pl.ds(r * pitch + LEAD - 1 + j, half, stride=2), :] for j in range(PLANES)
        ]

    window = [planes(0), planes(1)]
    for i in range(h // 2):
        window = window[-2:] + [planes(2 * i + 2), planes(2 * i + 3)]
        for j in range(PLANES):
            r0, r1, r2, r3 = (row[j] for row in window)
            for point, value in enumerate((r2 - r0, r1 + r2, r1 - r2, r1 - r3)):
                d[point, j, i * half : (i + 1) * half, :] = value.astype(BF16)


def taps(t, low, high):
    return lambda point: t[point, low:high].reshape(-1, t.shape[-1])


def products(pieces, right):
    m = []
    for point in range(POINTS):
        left = jnp.concatenate([p[point, j] for p in pieces for j in range(PLANES)], axis=1)
        m.append(jnp.dot(left, right(point), preferred_element_type=F32))
    return (m[1] - m[2]) - m[0], m[1] - (m[3] - m[2])


def live_phase(dims, odd, exists, multiplier, offset, bias_row, source, target, res, halos, s, d, t, acc, kept, emit):
    fr, cf, h, w, c = dims
    half = w // 2
    hr, hc, hk = halos
    multiplier, offset = 0.5 * multiplier, 0.5 * offset

    def act(values):
        return silu_of_half(values * multiplier + offset).astype(BF16)

    def masked(dy, dx, values):
        return jnp.where(exists(dy, dx), values.astype(F32), 0.0)

    def build_frame(f):
        def row_of(r):
            cells = act(source[f, r * w : (r + 1) * w, :])
            if f >= fr - cf:
                kept[f - (fr - cf), r * w : (r + 1) * w, :] = cells
            return cells.astype(F32)

        build(
            s.at[f],
            d.at[f],
            h,
            w,
            c,
            row_of,
            [lambda i=i: masked(SIDE[i], 0, act(hr[i, f].astype(F32))) for i in range(2)],
            [lambda i=i: masked(0, SIDE[i], act(hc[i, f].astype(F32))) for i in range(2)],
            [lambda i=i: masked(SIDE[i // 2], SIDE[i % 2], act(hk[i, f])) for i in range(4)],
        )

    zero = jnp.zeros((8, c), F32)
    sums, squares = zero, zero
    build_frame(0)
    for o in range(fr):
        first = max(0, o - cf)
        dt = first + cf - o
        both = products(
            [d.at[f] for f in range(first, o + 1)],
            taps(t, dt, cf + 1),
        )
        if o + 1 < fr:
            build_frame(o + 1)
        for q in range(2):
            y = both[q]
            if o < cf:
                y = y + acc[o, q]
            for i in range(h // 2):
                for e in range(2):
                    piece = y[i * half : (i + 1) * half, e * c : (e + 1) * c] + bias_row
                    at = pl.ds((2 * i + q) * w + e, half, stride=2)
                    if odd:
                        piece = (res[o, at, :] + piece).astype(BF16).astype(F32)
                    target[o, at, :] = piece
                    if emit is None:
                        slabs = piece.reshape(half // 8, 8, c)
                        sums = sums + jnp.sum(slabs, axis=0)
                        squares = squares + jnp.sum(slabs * slabs, axis=0)
        if emit is not None:
            emit(o)
    return sums, squares


def kernel(dims, *refs):
    (frames, caches, weights, bias_in, gain_in, shift_in,
     mid, res, acc, t_last, norm, hr_last, hc_last, hk_last, kept,
     x, cb, wv, s, d, dc, t, small,
     s_out, s_in,
     lr_out, lc_out, lk_out, lr_in, lc_in, lk_in,
     cr_out, cc_out, ck_out, cr_in, cc_in, ck_in,
     load_sem, weight_sem, small_sem,
     stat_send, stat_recv, halo_send, halo_recv) = refs
    nh, nw, fr, cf, convs, h, w, c = dims
    peers = nh * nw
    cell_count = fr * h * w * peers * (c // GROUPS)
    clip, ha, wa = lax.axis_index("clip"), lax.axis_index("ha"), lax.axis_index("wa")
    offsets = [(i, j) for i in range(nh) for j in range(nw) if (i, j) != (0, 0)]
    others = [(lax.rem(ha + i, nh), lax.rem(wa + j, nw)) for i, j in offsets]
    exists = exists_at(nh, nw)
    barrier = pltpu.get_barrier_semaphore()
    for ph, pw in others:
        pl.semaphore_signal(barrier, inc=1, device_id=(clip, ph, pw), device_id_type=MESH)

    load_x = pltpu.make_async_copy(frames, x, load_sem.at[0])
    load_x.start()

    def span(k):
        return pl.ds(0, 1) if k == 0 else pl.ds(1, convs - 1)

    def load_cache(k):
        return pltpu.make_async_copy(caches.at[:, span(k)], cb.at[:, span(k)], load_sem.at[1 + k])

    def load_weights(k):
        return pltpu.make_async_copy(weights.at[span(k)], wv.at[span(k)], weight_sem.at[k])

    small_copies = [
        pltpu.make_async_copy(ref, small.at[i], small_sem.at[i])
        for i, ref in enumerate((bias_in, gain_in, shift_in))
    ]
    for copy in small_copies:
        copy.start()
    for k in range(2):
        load_cache(k).start()
        load_weights(k).start()
    bias, gain, shift = small.at[0], small.at[1], small.at[2]

    def halo_copy(live, k, dy, dx, towards):
        inbox = (1, 3)[k % 2] if live else (0, 2)[k]
        outbox = int(live)
        group = span(k)
        rows_out, rows_in = (lr_out, lr_in) if live else (cr_out, cr_in)
        cols_out, cols_in = (lc_out, lc_in) if live else (cc_out, cc_in)
        ends_out, ends_in = (lk_out, lk_in) if live else (ck_out, ck_in)
        if dx == 0:
            src, dst = rows_out, rows_in
            near, far = int(dy > 0), int(dy < 0)
        elif dy == 0:
            src, dst = cols_out, cols_in
            near, far = int(dx > 0), int(dx < 0)
        else:
            src, dst = ends_out, ends_in
            near = int(dy > 0) * 2 + int(dx > 0)
            far = 3 - near
        if live:
            src, dst = src.at[k, near], dst.at[k, far]
        else:
            src, dst = src.at[near, group], dst.at[far, group]
        direction = DIRECTIONS.index((dy, dx))
        back = DIRECTIONS.index((-dy, -dx))
        return pltpu.make_async_remote_copy(
            src_ref=src,
            dst_ref=dst,
            send_sem=halo_send.at[outbox, direction],
            recv_sem=halo_recv.at[inbox, back],
            device_id=(clip, ha + dy * towards, wa + dx * towards),
            device_id_type=MESH,
        )

    def pack_edges(k, field):
        for f in range(fr):
            for side in range(2):
                first = side * (w - 1)
                top = side * (h - 1) * w
                lr_out[k, side, f] = field[f, top : top + w, :].astype(BF16)
                lc_out[k, side, f] = field[f, pl.ds(first, h, stride=w), :].astype(BF16)
                for low in range(2):
                    row = low * (h - 1) * w + first
                    lk_out[k, low * 2 + side, f] = field[f, row : row + 1, :]

    def send_halo(live, k):
        for dy, dx in DIRECTIONS:

            @pl.when(exists(dy, dx))
            def _():
                halo_copy(live, k, dy, dx, 1).start()

    def wait_halo(live, k):
        for dy, dx in DIRECTIONS:

            @pl.when(exists(dy, dx))
            def _():
                halo_copy(live, k, -dy, -dx, -1).wait_recv()

    def wait_sent(live, k):
        for dy, dx in DIRECTIONS:

            @pl.when(exists(dy, dx))
            def _():
                halo_copy(live, k, dy, dx, 1).wait_send()

    def send_stats(k, sums, squares):
        s_out[k] = jnp.concatenate(
            [jnp.sum(sums, axis=0, keepdims=True), jnp.sum(squares, axis=0, keepdims=True)], axis=0
        )
        for number, (ph, pw) in enumerate(others):
            pltpu.make_async_remote_copy(
                src_ref=s_out.at[k],
                dst_ref=s_in.at[k, number],
                send_sem=stat_send.at[0],
                recv_sem=stat_recv.at[k % 2],
                device_id=(clip, ph, pw),
                device_id_type=MESH,
            ).start()

    def all_stats(k, sem):
        return pltpu.make_async_copy(s_in.at[k], s_in.at[k], sem)

    def wait_stats(k):
        all_stats(k, stat_recv.at[k % 2]).wait()
        parts = [s_out[k]] + [s_in[k, i] for i in range(peers - 1)]
        while len(parts) > 1:
            parts = [
                parts[i] + parts[i + 1] if i + 1 < len(parts) else parts[i]
                for i in range(0, len(parts), 2)
            ]
        total = jnp.concatenate([parts[0], jnp.zeros((6, c), F32)], axis=0)
        lane = lax.broadcasted_iota(jnp.int32, (8, c), 1)
        step = 1
        while step < c // GROUPS:
            total = total + jnp.where(
                lax.rem(lane, 2 * step) < step,
                pltpu.roll(total, c - step, 1),
                pltpu.roll(total, step, 1),
            )
            step *= 2
        mean = total[0:1] / cell_count
        variance = total[1:2] / cell_count - mean * mean
        multiplier = lax.rsqrt(variance + EPSILON) * gain[k : k + 1, :]
        offset = shift[k : k + 1, :] - mean * multiplier
        return multiplier, offset

    def table(k):
        return t_last if k == convs - 1 else t.at[k % 2]

    def transform_weights(k):
        if k < 2:
            load_weights(k).wait()
        into = table(k)

        def body(dt, carry):
            for dw in range(3):
                rows = slice(dw * c, (dw + 1) * c)
                g = [wv[k, dt, dh, rows, :] for dh in range(3)]
                outer = g[0].astype(F32) + g[2].astype(F32)
                inner = g[1].astype(F32)
                values = (
                    g[0],
                    (0.5 * (outer + inner)).astype(BF16),
                    (0.5 * (outer - inner)).astype(BF16),
                    g[2],
                )
                for point in range(POINTS):
                    for e in range(2):
                        j = dw + e
                        into[point, dt, j * c : (j + 1) * c, e * c : (e + 1) * c] = values[point]
            for point in range(POINTS):
                into[point, dt, 3 * c : 4 * c, 0:c] = jnp.zeros((c, c), BF16)
                into[point, dt, 0:c, c : 2 * c] = jnp.zeros((c, c), BF16)
            return carry

        lax.fori_loop(0, 3, body, 0)

    def masked(dy, dx, values):
        return jnp.where(exists(dy, dx), values, 0.0)

    def cached_phase(k):
        for f in range(cf):
            build(
                s.at[f],
                dc.at[f],
                h,
                w,
                c,
                lambda r: cb[f, k, r * w : (r + 1) * w, :].astype(F32),
                [lambda i=i: masked(SIDE[i], 0, cr_in[i, k, f].astype(F32)) for i in range(2)],
                [lambda i=i: masked(0, SIDE[i], cc_in[i, k, f].astype(F32)) for i in range(2)],
                [lambda i=i: masked(SIDE[i // 2], SIDE[i % 2], ck_in[i, k, f]) for i in range(4)],
            )
        into = table(k)
        for o in range(cf):
            both = products(
                [dc.at[p] for p in range(o, cf)],
                taps(into, 0, cf - o),
            )
            for q in range(2):
                acc[o, q] = both[q]

    def pack_cached(k):
        if k < 2:
            load_cache(k).wait()

        for f in range(cf):
            for side in range(2):
                top = side * (h - 1) * w
                cr_out[side, k, f] = cb[f, k, top : top + w, :]
                s[f, 0 : h * w, :] = cb[f, k].astype(F32)
                first = side * (w - 1)
                cc_out[side, k, f] = s[f, pl.ds(first, h, stride=w), :].astype(BF16)
                for low in range(2):
                    row = low * (h - 1) * w + first
                    ck_out[low * 2 + side, k, f] = s[f, row : row + 1, :]

    def settle(k):
        wait_sent(True, k)
        all_stats(k, stat_send.at[0]).wait()

    load_x.wait()

    def widen(f, carry):
        sums, squares = carry
        values = x[f].astype(F32)
        res[f] = values
        slabs = values.reshape(h * w // 8, 8, c)
        return sums + jnp.sum(slabs, axis=0), squares + jnp.sum(slabs * slabs, axis=0)

    zero = jnp.zeros((8, c), F32)
    carry = lax.fori_loop(0, fr, widen, (zero, zero))
    pack_edges(0, res)
    pack_cached(0)
    pl.semaphore_wait(barrier, peers - 1)
    send_stats(0, *carry)
    send_halo(False, 0)
    transform_weights(0)
    send_halo(True, 0)
    for k in range(1, convs):
        pack_cached(k)
    wait_halo(False, 0)
    cached_phase(0)
    for copy in small_copies:
        copy.wait()
    last = convs - 1
    for k in range(convs):
        multiplier, offset = wait_stats(k)
        wait_halo(True, k)
        if k == last:
            break
        if k == 0:
            wait_sent(False, 0)
            send_halo(False, 1)
        source, target = (mid, res) if k % 2 else (res, mid)
        carry = live_phase(
            (fr, cf, h, w, c), k % 2, exists, multiplier, offset, bias[k : k + 1, :],
            source, target, res, (lr_in.at[k], lc_in.at[k], lk_in.at[k]),
            s, d, table(k), acc, kept.at[k], None,
        )
        settle(k)
        send_stats(k + 1, *carry)
        pack_edges(k + 1, target)
        send_halo(True, k + 1)
        transform_weights(k + 1)
        if k == 0:
            wait_halo(False, 1)
        cached_phase(k + 1)
        if k == 0:
            wait_sent(False, 1)

    norm[...] = jnp.zeros_like(norm)
    norm[0:1] = multiplier
    norm[1:2] = offset
    norm[2:3] = bias[last : last + 1, :]
    hr_last[...] = lr_in[last]
    hc_last[...] = lc_in[last]
    hk_last[...] = lk_in[last]
    settle(last)


def finish(dims, *refs):
    (mid, res, acc, t_last, norm_last, hr, hc, hk, kept,
     encoded, new_caches,
     s, d, out, kept_new, y, out_sem, kept_sem) = refs
    nh, nw, fr, cf, convs, h, w, c = dims
    exists = exists_at(nh, nw)
    copies = [
        pltpu.make_async_copy(kept.at[k], new_caches.at[:, k], kept_sem.at[k])
        for k in range(convs - 1)
    ]
    for copy in copies:
        copy.start()

    def emit(o):
        out[o] = y[o].astype(BF16)

    live_phase(
        (fr, cf, h, w, c), (convs - 1) % 2, exists, norm_last[0:1], norm_last[1:2], norm_last[2:3],
        mid, y, res, (hr, hc, hk), s, d, t_last, acc, kept_new, emit,
    )
    copies.append(
        pltpu.make_async_copy(kept_new, new_caches.at[:, convs - 1], kept_sem.at[convs - 1])
    )
    copies[-1].start()
    copies.append(pltpu.make_async_copy(out, encoded, out_sem.at[0]))
    copies[-1].start()
    for copy in copies:
        copy.wait()


def local(nh, nw, frames, caches, conv_weights, conv_bias, norm_gain, norm_shift):
    fr, h, w, c = frames.shape
    cf, convs = caches.shape[:2]
    dims = (nh, nw, fr, cf, convs, h, w, c)
    peers = nh * nw
    vmem = pltpu.VMEM
    dma = pltpu.SemaphoreType.DMA
    pitch = w + 2 * LEAD
    pairs = h * w // 4
    s_shape = vmem((fr, (h + 2) * pitch, c), F32)
    d_shape = vmem((fr, POINTS, PLANES, pairs, c), BF16)
    table = (POINTS, cf + 1, PLANES * c, 2 * c)
    scratch = [
        vmem((fr, h * w, c), BF16),
        vmem((cf, convs, h * w, c), BF16),
        vmem((convs, 3, 3, 3 * c, c), BF16),
        s_shape,
        d_shape,
        vmem((cf, POINTS, PLANES, pairs, c), BF16),
        vmem((2,) + table, BF16),
        vmem((3, convs, c), F32),
        vmem((convs, 2, c), F32),
        vmem((convs, peers - 1, 2, c), F32),
    ]
    for _ in range(2):
        scratch += [
            vmem((convs, 2, fr, w, c), BF16),
            vmem((convs, 2, fr, h, c), BF16),
            vmem((convs, 4, fr, 1, c), F32),
        ]
    for _ in range(2):
        scratch += [
            vmem((2, convs, cf, w, c), BF16),
            vmem((2, convs, cf, h, c), BF16),
            vmem((4, convs, cf, 1, c), F32),
        ]
    scratch += [
        dma((3,)),
        dma((2,)),
        dma((3,)),
        dma((1,)),
        dma((2,)),
        dma((2, 8)),
        dma((4, 8)),
    ]
    anywhere = pl.BlockSpec(memory_space=pltpu.HBM)
    inside = pl.BlockSpec(memory_space=pltpu.VMEM)
    handed = [
        ((fr, h * w, c), F32),
        ((fr, h * w, c), F32),
        ((cf, 2, pairs, 2 * c), F32),
        (table, BF16),
        ((8, c), F32),
        ((2, fr, w, c), BF16),
        ((2, fr, h, c), BF16),
        ((4, fr, 1, c), F32),
        ((convs - 1, cf, h * w, c), BF16),
    ]
    state = pl.pallas_call(
        functools.partial(kernel, dims),
        out_shape=[vmem(shape, dtype) for shape, dtype in handed],
        in_specs=[anywhere] * 6,
        out_specs=[inside] * len(handed),
        scratch_shapes=scratch,
        compiler_params=pltpu.CompilerParams(
            collective_id=0, has_side_effects=True, vmem_limit_bytes=48 * 1024 * 1024
        ),
    )(
        frames.reshape(fr, h * w, c),
        caches.reshape(cf, convs, h * w, c),
        conv_weights.reshape(convs, 3, 3, 3 * c, c),
        conv_bias,
        norm_gain,
        norm_shift,
    )
    encoded, new_caches = pl.pallas_call(
        functools.partial(finish, dims),
        out_shape=(
            jax.ShapeDtypeStruct((fr, h * w, c), BF16),
            jax.ShapeDtypeStruct((cf, convs, h * w, c), BF16),
        ),
        in_specs=[inside] * len(handed),
        out_specs=(anywhere, anywhere),
        scratch_shapes=[
            s_shape,
            d_shape,
            vmem((fr, h * w, c), BF16),
            vmem((cf, h * w, c), BF16),
            vmem((fr, h * w, c), F32),
            dma((1,)),
            dma((convs,)),
        ],
        compiler_params=pltpu.CompilerParams(vmem_limit_bytes=24 * 1024 * 1024),
    )(*state)
    return encoded.reshape(frames.shape), new_caches.reshape(caches.shape)


def solution(mesh):
    return jax.shard_map(
        functools.partial(local, mesh.shape["ha"], mesh.shape["wa"]),
        mesh=mesh,
        in_specs=(
            P("clip", "ha", "wa", None),
            P("clip", None, "ha", "wa", None),
            P(),
            P(),
            P(),
            P(),
        ),
        out_specs=(P("clip", "ha", "wa", None), P("clip", None, "ha", "wa", None)),
        check_vma=False,
    )
```

time: 51.1 us -> 38.7 us (0.76)
  Pallas kernels: 47 us -> 37.7 us
  local copies, waits for them, and re-layouts: 3.33 us -> 0 us
    pallas_call x1 -> x2, Pallas kernels: 47 us -> 37.7 us  [the longest x1 34.1 us: local(): pl.pallas_call(functools.partial(kernel, dims), out_shape=[vmem(shape, dt...]
    unnamed x4 -> x0, local copies, waits for them, and re-layouts: 3.33 us -> none
where the time goes in v1:
time: 38.7 us; the launch traced here: 38.5 us
  Pallas kernels  37.7 us (97%)
  between operations  0.8 us (2%)
    pallas_call x1, Pallas kernels, local(): pl.pallas_call(functools.partial(kernel, dims), out_shape=[vmem(shape, dt...  34.1 us
    pallas_call x1, Pallas kernels, local(): pl.pallas_call(functools.partial(finish, dims), out_shape=(jax.ShapeDtype...  3.67 us

profile of v1, /device:TPU:0, one launch (start us, length us, event | category | flops | bytes accessed | tf_op | source)
XLA Modules:
  0.0 38.5 jit_solution(4821755965613018150)
XLA Ops:
  0.6 34.1 %shard_map.77 = (f32[4,768,128]{2,1,0:T(8,128)S(1)}, f32[4,768,128]{2,1,0:T(8,128)S(1)}, f32[2,2,192,256]{3,2,1,0:T(8,128)S(1)}, bf16[4,3,512,256]{3,2,1,0:T(8,1...) custom-call(bf16[4,768,128]{2,1,0:T(8,128)(2,1)} %bitcast.7, ...), custom_call_target="tpu_custom_call" | custom-call | tf_op jit(solution)/shard_map/pallas_call | solution.py:514
  34.7 3.7 %shard_map.78 = (bf16[4,768,128]{2,1,0:T(8,128)(2,1)}, bf16[2,4,768,128]{3,2,1,0:T(8,128)(2,1)}) custom-call(f32[4,768,128]{2,1,0:T(8,128)S(1)} %get-tuple-element.13.refs_0_, f32[4,768,128]{2,1,0:T(8,128)S(1)} %get-tuple-element.14.refs_1_, f32[2,2,192,256]{3,2,1,0:T(8,128)S(1)} %get-tuple-element.15.refs_2_, ...), custom_call_target="tpu_custom_call" | custom-call | tf_op jit(solution)/shard_map/pallas_call | solution.py:531

commit v2 on v1

--- a/solution.py
+++ b/solution.py
@@ -69,15 +69,20 @@
     return lambda point: t[point, low:high].reshape(-1, t.shape[-1])
 
 
-def products(pieces, right):
+def products(pieces, right, before=None):
     m = []
     for point in range(POINTS):
         left = jnp.concatenate([p[point, j] for p in pieces for j in range(PLANES)], axis=1)
-        m.append(jnp.dot(left, right(point), preferred_element_type=F32))
+        value = jnp.dot(left, right(point), preferred_element_type=F32)
+        m.append(value if before is None else value + before[point])
+    return m
+
+
+def row_pair(m):
     return (m[1] - m[2]) - m[0], m[1] - (m[3] - m[2])
 
 
-def live_phase(dims, odd, exists, multiplier, offset, bias_row, source, target, res, halos, s, d, t, acc, kept, emit):
+def live_phase(dims, odd, exists, multiplier, offset, bias_row, source, target, halos, s, d, t, acc, kept, emit):
     fr, cf, h, w, c = dims
     half = w // 2
     hr, hc, hk = halos
@@ -111,25 +116,28 @@
     zero = jnp.zeros((8, c), F32)
     sums, squares = zero, zero
     build_frame(0)
+    before = None
     for o in range(fr):
-        first = max(0, o - cf)
-        dt = first + cf - o
-        both = products(
-            [d.at[f] for f in range(first, o + 1)],
-            taps(t, dt, cf + 1),
-        )
+        m = products([d.at[o]], taps(t, cf, cf + 1), before)
         if o + 1 < fr:
+            first = max(0, o + 1 - cf)
+            before = products(
+                [d.at[f] for f in range(first, o + 1)], taps(t, first + cf - o - 1, cf)
+            )
             build_frame(o + 1)
+        both = row_pair(m)
         for q in range(2):
             y = both[q]
-            if o < cf:
+            if odd or o < cf:
                 y = y + acc[o, q]
+            else:
+                y = y + jnp.concatenate([bias_row] * 2, axis=1)
             for i in range(h // 2):
                 for e in range(2):
-                    piece = y[i * half : (i + 1) * half, e * c : (e + 1) * c] + bias_row
+                    piece = y[i * half : (i + 1) * half, e * c : (e + 1) * c]
                     at = pl.ds((2 * i + q) * w + e, half, stride=2)
                     if odd:
-                        piece = (res[o, at, :] + piece).astype(BF16).astype(F32)
+                        piece = piece.astype(BF16).astype(F32)
                     target[o, at, :] = piece
                     if emit is None:
                         slabs = piece.reshape(half // 8, 8, c)
@@ -142,8 +150,8 @@
 
 def kernel(dims, *refs):
     (frames, caches, weights, bias_in, gain_in, shift_in,
-     mid, res, acc, t_last, norm, hr_last, hc_last, hk_last, kept,
-     x, cb, wv, s, d, dc, t, small,
+     mid, acc, t_last, norm, hr_last, hc_last, hk_last, kept,
+     res, x, cb, wv, s, d, dc, t, small,
      s_out, s_in,
      lr_out, lc_out, lk_out, lr_in, lc_in, lk_in,
      cr_out, cc_out, ck_out, cr_in, cc_in, ck_in,
@@ -173,7 +181,7 @@
         return pltpu.make_async_copy(weights.at[span(k)], wv.at[span(k)], weight_sem.at[k])
 
     small_copies = [
-        pltpu.make_async_copy(ref, small.at[i], small_sem.at[i])
+        pltpu.make_async_copy(ref, small.at[i], small_sem.at[0])
         for i, ref in enumerate((bias_in, gain_in, shift_in))
     ]
     for copy in small_copies:
@@ -336,13 +344,22 @@
                 [lambda i=i: masked(SIDE[i // 2], SIDE[i % 2], ck_in[i, k, f]) for i in range(4)],
             )
         into = table(k)
-        for o in range(cf):
-            both = products(
-                [dc.at[p] for p in range(o, cf)],
-                taps(into, 0, cf - o),
-            )
+        row = bias[k : k + 1, :]
+        half = w // 2
+        for o in range(fr if k % 2 else cf):
+            if o < cf:
+                both = row_pair(products([dc.at[p] for p in range(o, cf)], taps(into, 0, cf - o)))
             for q in range(2):
-                acc[o, q] = both[q]
+                for i in range(h // 2):
+                    for e in range(2):
+                        rows, lanes = slice(i * half, (i + 1) * half), slice(e * c, (e + 1) * c)
+                        piece = row
+                        if o < cf:
+                            piece = piece + both[q][rows, lanes]
+                        if k % 2:
+                            at = pl.ds((2 * i + q) * w + e, half, stride=2)
+                            piece = piece + res[o, at, :]
+                        acc[o, q, rows, lanes] = piece
 
     def pack_cached(k):
         if k < 2:
@@ -383,10 +400,9 @@
     send_halo(True, 0)
     for k in range(1, convs):
         pack_cached(k)
+    pltpu.make_async_copy(small, small, small_sem.at[0]).wait()
     wait_halo(False, 0)
     cached_phase(0)
-    for copy in small_copies:
-        copy.wait()
     last = convs - 1
     for k in range(convs):
         multiplier, offset = wait_stats(k)
@@ -399,7 +415,7 @@
         source, target = (mid, res) if k % 2 else (res, mid)
         carry = live_phase(
             (fr, cf, h, w, c), k % 2, exists, multiplier, offset, bias[k : k + 1, :],
-            source, target, res, (lr_in.at[k], lc_in.at[k], lk_in.at[k]),
+            source, target, (lr_in.at[k], lc_in.at[k], lk_in.at[k]),
             s, d, table(k), acc, kept.at[k], None,
         )
         settle(k)
@@ -424,7 +440,7 @@
 
 
 def finish(dims, *refs):
-    (mid, res, acc, t_last, norm_last, hr, hc, hk, kept,
+    (mid, acc, t_last, norm_last, hr, hc, hk, kept,
      encoded, new_caches,
      s, d, out, kept_new, y, out_sem, kept_sem) = refs
     nh, nw, fr, cf, convs, h, w, c = dims
@@ -441,7 +457,7 @@
 
     live_phase(
         (fr, cf, h, w, c), (convs - 1) % 2, exists, norm_last[0:1], norm_last[1:2], norm_last[2:3],
-        mid, y, res, (hr, hc, hk), s, d, t_last, acc, kept_new, emit,
+        mid, y, (hr, hc, hk), s, d, t_last, acc, kept_new, emit,
     )
     copies.append(
         pltpu.make_async_copy(kept_new, new_caches.at[:, convs - 1], kept_sem.at[convs - 1])
@@ -466,6 +482,7 @@
     d_shape = vmem((fr, POINTS, PLANES, pairs, c), BF16)
     table = (POINTS, cf + 1, PLANES * c, 2 * c)
     scratch = [
+        vmem((fr, h * w, c), F32),
         vmem((fr, h * w, c), BF16),
         vmem((cf, convs, h * w, c), BF16),
         vmem((convs, 3, 3, 3 * c, c), BF16),
@@ -492,7 +509,7 @@
     scratch += [
         dma((3,)),
         dma((2,)),
-        dma((3,)),
+        dma((1,)),
         dma((1,)),
         dma((2,)),
         dma((2, 8)),
@@ -502,8 +519,7 @@
     inside = pl.BlockSpec(memory_space=pltpu.VMEM)
     handed = [
         ((fr, h * w, c), F32),
-        ((fr, h * w, c), F32),
-        ((cf, 2, pairs, 2 * c), F32),
+        ((fr, 2, pairs, 2 * c), F32),
         (table, BF16),
         ((8, c), F32),
         ((2, fr, w, c), BF16),

time: 38.7 us -> 38 us (0.982)
  Pallas kernels: 37.7 us -> 37 us
    pallas_call x1, Pallas kernels: 34.1 us -> 33.6 us  [local(): pl.pallas_call(functools.partial(kernel, dims), out_shape=[vmem(shape, dt...]
where the time goes in v2:
time: 38 us; the launch traced here: 37.8 us
  Pallas kernels  37 us (97%)
  between operations  0.8 us (2%)
    pallas_call x1, Pallas kernels, local(): pl.pallas_call(functools.partial(kernel, dims), out_shape=[vmem(shape, dt...  33.6 us
    pallas_call x1, Pallas kernels, local(): pl.pallas_call(functools.partial(finish, dims), out_shape=(jax.ShapeDtype...  3.46 us

profile of v2, /device:TPU:0, one launch (start us, length us, event | category | flops | bytes accessed | tf_op | source)
XLA Modules:
  0.0 37.8 jit_solution(13175665018407108917)
XLA Ops:
  0.6 33.6 %shard_map.77 = (f32[4,768,128]{2,1,0:T(8,128)S(1)}, f32[4,2,192,256]{3,2,1,0:T(8,128)S(1)}, bf16[4,3,512,256]{3,2,1,0:T(8,128)(2,1)S(1)}, f32[8,128]{1,0:T(8,12...) custom-call(bf16[4,768,128]{2,1,0:T(8,128)(2,1)} %bitcast.7, ...), custom_call_target="tpu_custom_call" | custom-call | tf_op jit(solution)/shard_map/pallas_call | solution.py:530
  34.2 3.5 %shard_map.78 = (bf16[4,768,128]{2,1,0:T(8,128)(2,1)}, bf16[2,4,768,128]{3,2,1,0:T(8,128)(2,1)}) custom-call(f32[4,768,128]{2,1,0:T(8,128)S(1)} %get-tuple-element.12.refs_0_, f32[4,2,192,256]{3,2,1,0:T(8,128)S(1)} %get-tuple-element.13.refs_1_, bf16[4,3,512,256]{3,2,1,0:T(8,128)(2,1)S(1)} %get-tuple-element.14.refs_2_, ...), custom_call_target="tpu_custom_call" | custom-call | tf_op jit(solution)/shard_map/pallas_call | solution.py:547

commit v3 on v2

--- a/solution.py
+++ b/solution.py
@@ -161,7 +161,10 @@
     peers = nh * nw
     cell_count = fr * h * w * peers * (c // GROUPS)
     clip, ha, wa = lax.axis_index("clip"), lax.axis_index("ha"), lax.axis_index("wa")
-    offsets = [(i, j) for i in range(nh) for j in range(nw) if (i, j) != (0, 0)]
+    offsets = sorted(
+        ((i, j) for i in range(nh) for j in range(nw) if (i, j) != (0, 0)),
+        key=lambda ij: -sum((x % 2) * 2 + (x > 0) for x in ij),
+    )
     others = [(lax.rem(ha + i, nh), lax.rem(wa + j, nw)) for i, j in offsets]
     exists = exists_at(nh, nw)
     barrier = pltpu.get_barrier_semaphore()
@@ -280,16 +283,13 @@
                 parts[i] + parts[i + 1] if i + 1 < len(parts) else parts[i]
                 for i in range(0, len(parts), 2)
             ]
-        total = jnp.concatenate([parts[0], jnp.zeros((6, c), F32)], axis=0)
-        lane = lax.broadcasted_iota(jnp.int32, (8, c), 1)
-        step = 1
-        while step < c // GROUPS:
-            total = total + jnp.where(
-                lax.rem(lane, 2 * step) < step,
-                pltpu.roll(total, c - step, 1),
-                pltpu.roll(total, step, 1),
-            )
-            step *= 2
+        rows = jnp.concatenate([parts[0], jnp.zeros((6, c), F32)], axis=0)
+        size = c // GROUPS
+        place = lax.rem(lax.broadcasted_iota(jnp.int32, (8, c), 1), size)
+        total = rows
+        for step in range(1, size):
+            total = total + jnp.where(place + step < size, pltpu.roll(rows, c - step, 1), 0.0)
+            total = total + jnp.where(place >= step, pltpu.roll(rows, step, 1), 0.0)
         mean = total[0:1] / cell_count
         variance = total[1:2] / cell_count - mean * mean
         multiplier = lax.rsqrt(variance + EPSILON) * gain[k : k + 1, :]
@@ -403,14 +403,15 @@
     pltpu.make_async_copy(small, small, small_sem.at[0]).wait()
     wait_halo(False, 0)
     cached_phase(0)
+    wait_sent(False, 0)
     last = convs - 1
+    settle(0)
     for k in range(convs):
         multiplier, offset = wait_stats(k)
         wait_halo(True, k)
         if k == last:
             break
         if k == 0:
-            wait_sent(False, 0)
             send_halo(False, 1)
         source, target = (mid, res) if k % 2 else (res, mid)
         carry = live_phase(
@@ -418,7 +419,6 @@
             source, target, (lr_in.at[k], lc_in.at[k], lk_in.at[k]),
             s, d, table(k), acc, kept.at[k], None,
         )
-        settle(k)
         send_stats(k + 1, *carry)
         pack_edges(k + 1, target)
         send_halo(True, k + 1)
@@ -428,6 +428,7 @@
         cached_phase(k + 1)
         if k == 0:
             wait_sent(False, 1)
+        settle(k + 1)
 
     norm[...] = jnp.zeros_like(norm)
     norm[0:1] = multiplier
@@ -436,7 +437,6 @@
     hr_last[...] = lr_in[last]
     hc_last[...] = lc_in[last]
     hk_last[...] = lk_in[last]
-    settle(last)
 
 
 def finish(dims, *refs):

time: 38 us -> 37.5 us (0.987)
  Pallas kernels: 37 us -> 36.5 us
    pallas_call x1, Pallas kernels: 33.6 us -> 33.1 us  [local(): pl.pallas_call(functools.partial(kernel, dims), out_shape=[vmem(shape, dt...]
where the time goes in v3:
time: 37.5 us; the launch traced here: 37.3 us
  Pallas kernels  36.5 us (97%)
  between operations  0.8 us (2%)
    pallas_call x1, Pallas kernels, local(): pl.pallas_call(functools.partial(kernel, dims), out_shape=[vmem(shape, dt...  33.1 us
    pallas_call x1, Pallas kernels, local(): pl.pallas_call(functools.partial(finish, dims), out_shape=(jax.ShapeDtype...  3.46 us

profile of v3, /device:TPU:0, one launch (start us, length us, event | category | flops | bytes accessed | tf_op | source)
XLA Modules:
  0.0 37.3 jit_solution(973356939979777840)
XLA Ops:
  0.6 33.1 %shard_map.77 = (f32[4,768,128]{2,1,0:T(8,128)S(1)}, f32[4,2,192,256]{3,2,1,0:T(8,128)S(1)}, bf16[4,3,512,256]{3,2,1,0:T(8,128)(2,1)S(1)}, f32[8,128]{1,0:T(8,12...) custom-call(bf16[4,768,128]{2,1,0:T(8,128)(2,1)} %bitcast.7, ...), custom_call_target="tpu_custom_call" | custom-call | tf_op jit(solution)/shard_map/pallas_call | solution.py:530
  33.7 3.5 %shard_map.78 = (bf16[4,768,128]{2,1,0:T(8,128)(2,1)}, bf16[2,4,768,128]{3,2,1,0:T(8,128)(2,1)}) custom-call(f32[4,768,128]{2,1,0:T(8,128)S(1)} %get-tuple-element.12.refs_0_, f32[4,2,192,256]{3,2,1,0:T(8,128)S(1)} %get-tuple-element.13.refs_1_, bf16[4,3,512,256]{3,2,1,0:T(8,128)(2,1)S(1)} %get-tuple-element.14.refs_2_, ...), custom_call_target="tpu_custom_call" | custom-call | tf_op jit(solution)/shard_map/pallas_call | solution.py:547

commit v4 on v3

--- a/solution.py
+++ b/solution.py
@@ -82,7 +82,7 @@
     return (m[1] - m[2]) - m[0], m[1] - (m[3] - m[2])
 
 
-def live_phase(dims, odd, exists, multiplier, offset, bias_row, source, target, halos, s, d, t, acc, kept, emit):
+def live_phase(dims, odd, exists, multiplier, offset, bias_row, source, target, halos, s, d, t, acc, kept, emit, midway=None):
     fr, cf, h, w, c = dims
     half = w // 2
     hr, hc, hk = halos
@@ -118,6 +118,8 @@
     build_frame(0)
     before = None
     for o in range(fr):
+        if o == fr - 1 and midway is not None:
+            midway()
         m = products([d.at[o]], taps(t, cf, cf + 1), before)
         if o + 1 < fr:
             first = max(0, o + 1 - cf)
@@ -196,7 +198,6 @@
 
     def halo_copy(live, k, dy, dx, towards):
         inbox = (1, 3)[k % 2] if live else (0, 2)[k]
-        outbox = int(live)
         group = span(k)
         rows_out, rows_in = (lr_out, lr_in) if live else (cr_out, cr_in)
         cols_out, cols_in = (lc_out, lc_in) if live else (cc_out, cc_in)
@@ -220,7 +221,7 @@
         return pltpu.make_async_remote_copy(
             src_ref=src,
             dst_ref=dst,
-            send_sem=halo_send.at[outbox, direction],
+            send_sem=halo_send.at[direction],
             recv_sem=halo_recv.at[inbox, back],
             device_id=(clip, ha + dy * towards, wa + dx * towards),
             device_id_type=MESH,
@@ -397,13 +398,13 @@
     send_stats(0, *carry)
     send_halo(False, 0)
     transform_weights(0)
-    send_halo(True, 0)
     for k in range(1, convs):
         pack_cached(k)
+    wait_sent(False, 0)
+    send_halo(True, 0)
     pltpu.make_async_copy(small, small, small_sem.at[0]).wait()
     wait_halo(False, 0)
     cached_phase(0)
-    wait_sent(False, 0)
     last = convs - 1
     settle(0)
     for k in range(convs):
@@ -421,13 +422,13 @@
         )
         send_stats(k + 1, *carry)
         pack_edges(k + 1, target)
+        if k == 0:
+            wait_sent(False, 1)
         send_halo(True, k + 1)
         transform_weights(k + 1)
         if k == 0:
             wait_halo(False, 1)
         cached_phase(k + 1)
-        if k == 0:
-            wait_sent(False, 1)
         settle(k + 1)
 
     norm[...] = jnp.zeros_like(norm)
@@ -442,7 +443,7 @@
 def finish(dims, *refs):
     (mid, acc, t_last, norm_last, hr, hc, hk, kept,
      encoded, new_caches,
-     s, d, out, kept_new, y, out_sem, kept_sem) = refs
+     s, d, out_first, out_last, kept_new, y, out_sem, kept_sem) = refs
     nh, nw, fr, cf, convs, h, w, c = dims
     exists = exists_at(nh, nw)
     copies = [
@@ -452,19 +453,27 @@
     for copy in copies:
         copy.start()
 
+    early = out_first.shape[0]
+
     def emit(o):
-        out[o] = y[o].astype(BF16)
+        if o < early:
+            out_first[o] = y[o].astype(BF16)
+        else:
+            out_last[o - early] = y[o].astype(BF16)
+
+    def send_out(source, into, sem):
+        copies.append(pltpu.make_async_copy(source, into, sem))
+        copies[-1].start()
+
+    def midway():
+        send_out(kept_new, new_caches.at[:, convs - 1], kept_sem.at[convs - 1])
+        send_out(out_first, encoded.at[pl.ds(0, early)], out_sem.at[0])
 
     live_phase(
         (fr, cf, h, w, c), (convs - 1) % 2, exists, norm_last[0:1], norm_last[1:2], norm_last[2:3],
-        mid, y, (hr, hc, hk), s, d, t_last, acc, kept_new, emit,
+        mid, y, (hr, hc, hk), s, d, t_last, acc, kept_new, emit, midway,
     )
-    copies.append(
-        pltpu.make_async_copy(kept_new, new_caches.at[:, convs - 1], kept_sem.at[convs - 1])
-    )
-    copies[-1].start()
-    copies.append(pltpu.make_async_copy(out, encoded, out_sem.at[0]))
-    copies[-1].start()
+    send_out(out_last, encoded.at[pl.ds(early, fr - early)], out_sem.at[1])
     for copy in copies:
         copy.wait()
 
@@ -512,7 +521,7 @@
         dma((1,)),
         dma((1,)),
         dma((2,)),
-        dma((2, 8)),
+        dma((8,)),
         dma((4, 8)),
     ]
     anywhere = pl.BlockSpec(memory_space=pltpu.HBM)
@@ -555,10 +564,11 @@
         scratch_shapes=[
             s_shape,
             d_shape,
-            vmem((fr, h * w, c), BF16),
+            vmem((fr - 2, h * w, c), BF16),
+            vmem((2, h * w, c), BF16),
             vmem((cf, h * w, c), BF16),
             vmem((fr, h * w, c), F32),
-            dma((1,)),
+            dma((2,)),
             dma((convs,)),
         ],
         compiler_params=pltpu.CompilerParams(vmem_limit_bytes=24 * 1024 * 1024),

time: 37.5 us -> 37.4 us (level)
  no operation moved by 1% of the time
where the time goes in v4:
time: 37.4 us; the launch traced here: 37.2 us
  Pallas kernels  36.4 us (97%)
  between operations  0.8 us (2%)
    pallas_call x1, Pallas kernels, local(): pl.pallas_call(functools.partial(kernel, dims), out_shape=[vmem(shape, dt...  33.1 us
    pallas_call x1, Pallas kernels, local(): pl.pallas_call(functools.partial(finish, dims), out_shape=(jax.ShapeDtype...  3.35 us

profile of v4, /device:TPU:0, one launch (start us, length us, event | category | flops | bytes accessed | tf_op | source)
XLA Modules:
  0.0 37.2 jit_solution(851527506802597289)
XLA Ops:
  0.6 33.1 %shard_map.77 = (f32[4,768,128]{2,1,0:T(8,128)S(1)}, f32[4,2,192,256]{3,2,1,0:T(8,128)S(1)}, bf16[4,3,512,256]{3,2,1,0:T(8,128)(2,1)S(1)}, f32[8,128]{1,0:T(8,12...) custom-call(bf16[4,768,128]{2,1,0:T(8,128)(2,1)} %bitcast.7, ...), custom_call_target="tpu_custom_call" | custom-call | tf_op jit(solution)/shard_map/pallas_call | solution.py:539
  33.7 3.4 %shard_map.78 = (bf16[4,768,128]{2,1,0:T(8,128)(2,1)}, bf16[2,4,768,128]{3,2,1,0:T(8,128)(2,1)}) custom-call(f32[4,768,128]{2,1,0:T(8,128)S(1)} %get-tuple-element.12.refs_0_, f32[4,2,192,256]{3,2,1,0:T(8,128)S(1)} %get-tuple-element.13.refs_1_, bf16[4,3,512,256]{3,2,1,0:T(8,128)(2,1)S(1)} %get-tuple-element.14.refs_2_, ...), custom_call_target="tpu_custom_call" | custom-call | tf_op jit(solution)/shard_map/pallas_call | solution.py:556

commit v5 on v4

--- a/solution.py
+++ b/solution.py
@@ -421,11 +421,11 @@
             s, d, table(k), acc, kept.at[k], None,
         )
         send_stats(k + 1, *carry)
+        transform_weights(k + 1)
         pack_edges(k + 1, target)
         if k == 0:
             wait_sent(False, 1)
         send_halo(True, k + 1)
-        transform_weights(k + 1)
         if k == 0:
             wait_halo(False, 1)
         cached_phase(k + 1)

time: 37.4 us -> 37.5 us (level)
  no operation moved by 1% of the time
where the time goes in v5:
time: 37.5 us; the launch traced here: 37.4 us
  Pallas kernels  36.6 us (98%)
  between operations  0.8 us (2%)
    pallas_call x1, Pallas kernels, local(): pl.pallas_call(functools.partial(kernel, dims), out_shape=[vmem(shape, dt...  33.3 us
    pallas_call x1, Pallas kernels, local(): pl.pallas_call(functools.partial(finish, dims), out_shape=(jax.ShapeDtype...  3.35 us

profile of v5, /device:TPU:0, one launch (start us, length us, event | category | flops | bytes accessed | tf_op | source)
XLA Modules:
  0.0 37.4 jit_solution(14665145793785806603)
XLA Ops:
  0.6 33.3 %shard_map.77 = (f32[4,768,128]{2,1,0:T(8,128)S(1)}, f32[4,2,192,256]{3,2,1,0:T(8,128)S(1)}, bf16[4,3,512,256]{3,2,1,0:T(8,128)(2,1)S(1)}, f32[8,128]{1,0:T(8,12...) custom-call(bf16[4,768,128]{2,1,0:T(8,128)(2,1)} %bitcast.7, ...), custom_call_target="tpu_custom_call" | custom-call | tf_op jit(solution)/shard_map/pallas_call | solution.py:539
  33.9 3.4 %shard_map.78 = (bf16[4,768,128]{2,1,0:T(8,128)(2,1)}, bf16[2,4,768,128]{3,2,1,0:T(8,128)(2,1)}) custom-call(f32[4,768,128]{2,1,0:T(8,128)S(1)} %get-tuple-element.12.refs_0_, f32[4,2,192,256]{3,2,1,0:T(8,128)S(1)} %get-tuple-element.13.refs_1_, bf16[4,3,512,256]{3,2,1,0:T(8,128)(2,1)S(1)} %get-tuple-element.14.refs_2_, ...), custom_call_target="tpu_custom_call" | custom-call | tf_op jit(solution)/shard_map/pallas_call | solution.py:556
